TPU v7x, 32 devices: a 4x4x1 block of a 4x4x8 slice. The times are simulated.
32 devices in a mesh: batch: 1 (over z), row: 4 (over y), col: 8 (over x, core).
Axes of the slice: x: 4, y: 4, z: 1, core: 2. Of those that a mesh axis runs over, the one named last changes fastest.
The devices are a block of a 4x4x8 slice.
Arguments:
- spd_blocks: float32 [64, 128, 8192], P(('batch', 'row'), None, 'col')
Outputs:
- output: float32 [64, 128, 8192], P(('batch', 'row'), None, 'col')
All inputs are finite; a program needn't handle non-finite values.
Results may differ from a plain program's by a relative error of at most 0.001.
Values are sent between devices in bfloat16 or wider.
A program may use at most 768 MiB of HBM per device.

v0:
```python
import functools
import jax
import jax.numpy as jnp
from jax import lax
from jax.sharding import PartitionSpec as P, NamedSharding


def transposed_panel(row_panel, row_id, col_id, row_devs, col_devs, row_skip, col_skip):
    row_blocks = row_panel.shape[0]
    blk_size = row_panel.shape[1]
    if row_devs >= col_devs:
        grid_ratio = row_devs // col_devs
        blk_shift = (row_skip * row_devs - col_skip * col_devs) // col_devs
        pick_mask = (jnp.arange(grid_ratio) == row_id // col_devs) & (row_id % col_devs == col_id)
        spread = (row_panel[:, None] * pick_mask.astype(jnp.bfloat16)[None, :, None, None]).reshape(row_blocks * grid_ratio, blk_size, blk_size)
        if blk_shift >= 0:
            spread = jnp.pad(spread, ((blk_shift, 0), (0, 0), (0, 0)))
        else:
            spread = spread[-blk_shift:]
    else:
        grid_ratio = col_devs // row_devs
        blk_shift = (col_skip * col_devs - row_skip * row_devs) // row_devs
        if blk_shift >= 0:
            shifted = row_panel[blk_shift:]
        else:
            shifted = jnp.pad(row_panel, ((-blk_shift, 0), (0, 0), (0, 0)))
        grouped = shifted.reshape(shifted.shape[0] // grid_ratio, grid_ratio, blk_size, blk_size)
        chosen = lax.dynamic_index_in_dim(grouped, col_id // row_devs, axis=1, keepdims=False)
        spread = jnp.where(row_id == col_id % row_devs, chosen, jnp.zeros_like(chosen))
    return lax.psum(spread, "row")


def solution(mesh):
    row_devs = mesh.shape["row"]
    col_devs = mesh.shape["col"]

    def factor_local(a_loc):
        row_blocks, blk_size, local_cols = a_loc.shape
        col_blocks = local_cols // blk_size
        blk_count = row_blocks * row_devs
        row_id = lax.axis_index("row")
        col_id = lax.axis_index("col")
        eye_blk = jnp.eye(blk_size, dtype=jnp.float32)

        def panel_step(step_idx, window):
            win_rows, win_cols = window.shape
            win_rblk = win_rows // blk_size
            row_skip = row_blocks - win_rblk
            col_skip = col_blocks - win_cols // blk_size
            own_col = col_id == step_idx % col_devs
            is_owner = own_col & (row_id == step_idx % row_devs)
            col_off = (step_idx // col_devs - col_skip) * blk_size
            col_blk = lax.dynamic_slice_in_dim(window, col_off, blk_size, axis=1)
            diag_blk = lax.dynamic_slice_in_dim(col_blk, (step_idx // row_devs - row_skip) * blk_size, blk_size, axis=0)
            diag_own = jnp.tril(jnp.linalg.cholesky(jnp.where(is_owner, diag_blk, eye_blk)))
            diag_fac = lax.psum(jnp.where(is_owner, diag_own, 0.0), "row")
            diag_fac = jnp.where(own_col, diag_fac, eye_blk)
            solved = lax.linalg.triangular_solve(diag_fac, col_blk, left_side=False, lower=True, transpose_a=True)
            row_ids = (row_skip + jnp.arange(win_rblk)) * row_devs + row_id
            below_mask = (row_ids > step_idx)[:, None, None]
            on_diag = (row_ids == step_idx)[:, None, None]
            solved_blocks = solved.reshape(win_rblk, blk_size, blk_size)
            prior_col = col_blk.reshape(win_rblk, blk_size, blk_size)
            new_col = jnp.where(below_mask, solved_blocks, jnp.where(on_diag, diag_fac[None], prior_col))
            new_col = jnp.where(own_col, new_col, prior_col).reshape(win_rows, blk_size)
            window = lax.dynamic_update_slice_in_dim(window, new_col, col_off, axis=1)
            row_panel = lax.psum(jnp.where(below_mask & own_col, solved_blocks, 0.0).astype(jnp.bfloat16), "col")
            col_panel = transposed_panel(row_panel, row_id, col_id, row_devs, col_devs, row_skip, col_skip)
            update = lax.dot_general(row_panel.reshape(win_rows, blk_size), col_panel.reshape(win_cols, blk_size), (((1,), (1,)), ((), ())), preferred_element_type=jnp.float32)
            return window - update

        work_mat = a_loc.reshape(row_blocks * blk_size, local_cols)
        phase_count = min(blk_count, 8)
        bounds = [(phase_idx * blk_count) // phase_count for phase_idx in range(phase_count + 1)]
        for phase_idx in range(phase_count):
            row_start = (bounds[phase_idx] // row_devs) * blk_size
            col_start = (bounds[phase_idx] // col_devs) * blk_size
            window = lax.fori_loop(bounds[phase_idx], bounds[phase_idx + 1], panel_step, work_mat[row_start:, col_start:])
            work_mat = lax.dynamic_update_slice(work_mat, window, (row_start, col_start))
        row_blk_ids = jnp.arange(row_blocks) * row_devs + row_id
        col_blk_ids = jnp.arange(col_blocks) * col_devs + col_id
        keep_mask = row_blk_ids[:, None, None, None] >= col_blk_ids[None, None, :, None]
        factor = jnp.where(keep_mask, work_mat.reshape(row_blocks, blk_size, col_blocks, blk_size), 0.0)
        return factor.reshape(row_blocks, blk_size, local_cols)

    blk_spec = P(("batch", "row"), None, "col")
    return jax.shard_map(factor_local, mesh=mesh, in_specs=(blk_spec,), out_specs=blk_spec, check_vma=False)
```

profile of v0, /device:TPU:97, one launch (start us, length us, event | category | flops | bytes accessed | tf_op | source)
XLA Modules:
  0.0 10166.7 jit_solution(8441392734871503061)
XLA Ops:
  15.0 1340.5 %while.152 = (s32[]{:T(128)}, f32[2048,1024]{1,0:T(8,128)}, s32[]{:T(128)}, s32[]{:T(128)}, pred[]{:T(512)}, /*index=5*/s32[]{:T(128)}, s32[]{:T(128)}, s32[]{:T...) while((s32[]{:T(128)}, f32[2048,1024]{1,0:T(8,128)}, ...), condition=%wide.region_6.8_spmd.clone.clone, body=%wide.region_0.7_spmd.clone.clone.sunk | while | flops 943816960 | bytes 32179992 | solution.py:78
  81.1 56.0 all-reduce.26.cloned.1.call-done
  415.6 56.0 all-reduce.26.cloned.1.call-done
  582.8 56.1 all-reduce.26.cloned.1.call-done
  750.0 56.9 all-reduce.26.cloned.1.call-done
  918.0 56.0 all-reduce.26.cloned.1.call-done
  1085.1 56.6 all-reduce.26.cloned.1.call-done
  1253.0 56.1 all-reduce.26.cloned.1.call-done
  1361.4 1325.2 %while.153 = (s32[]{:T(128)}, f32[1792,896]{1,0:T(8,128)}, s32[]{:T(128)}, s32[]{:T(128)}, pred[]{:T(512)}, /*index=5*/s32[]{:T(128)}, s32[]{:T(128)}, s32[]{:T(...) while((s32[]{:T(128)}, f32[1792,896]{1,0:T(8,128)}, ...), condition=%wide.region_11.13_spmd.clone.clone, body=%wide.region_7.12_spmd.clone.clone.sunk | while | flops 766935296 | bytes 26511272 | solution.py:78
  1426.4 56.0 all-reduce.32.cloned.1.call-done
  1757.2 56.0 all-reduce.32.cloned.1.call-done
  1922.6 56.0 all-reduce.32.cloned.1.call-done
  2088.0 56.8 all-reduce.32.cloned.1.call-done
  2254.2 56.0 all-reduce.32.cloned.1.call-done
  2419.8 56.5 all-reduce.32.cloned.1.call-done
  2585.8 56.0 all-reduce.32.cloned.1.call-done
  2697.5 1311.9 %while.154 = (s32[]{:T(128)}, f32[1536,768]{1,0:T(8,128)}, s32[]{:T(128)}, s32[]{:T(128)}, pred[]{:T(512)}, /*index=5*/s32[]{:T(128)}, s32[]{:T(128)}, s32[]{:T(...) while((s32[]{:T(128)}, f32[1536,768]{1,0:T(8,128)}, ...), condition=%wide.region_16.18_spmd.clone.clone, body=%wide.region_12.17_spmd.clone.clone.sunk | while | flops 606896384 | bytes 21366700 | solution.py:78
  2762.2 55.8 all-reduce.38.cloned.1.call-done
  3089.7 55.8 all-reduce.38.cloned.1.call-done
  3253.5 55.8 all-reduce.38.cloned.1.call-done
  3417.4 56.7 all-reduce.38.cloned.1.call-done
  3745.6 56.4 all-reduce.38.cloned.1.call-done
  4016.3 1280.5 %while.155 = (s32[]{:T(128)}, f32[1280,640]{1,0:T(8,128)S(1)}, s32[]{:T(128)}, s32[]{:T(128)}, pred[]{:T(512)}, /*index=5*/s32[]{:T(128)}, s32[]{:T(128)}, s32[]...) while((s32[]{:T(128)}, f32[1280,640]{1,0:T(8,128)S(1)}, ...), condition=%wide.region_21.23_spmd.clone.clone, body=%wide.region_17.22_spmd.clone.clone.sunk | while | flops 463700224 | bytes 16746402 | solution.py:78
  4720.8 56.4 all-reduce.44.cloned.1.call-done
  5041.3 56.1 all-reduce.44.cloned.1.call-done
  5300.4 1282.8 %while.156 = (s32[]{:T(128)}, f32[1024,512]{1,0:T(8,128)}, s32[]{:T(128)}, s32[]{:T(128)}, pred[]{:T(512)}, /*index=5*/s32[]{:T(128)}, s32[]{:T(128)}, s32[]{:T(...) while((s32[]{:T(128)}, f32[1024,512]{1,0:T(8,128)}, ...), condition=%wide.region_26.28_spmd.clone.clone, body=%wide.region_22.27_spmd.clone.clone.sunk | while | flops 337346784 | bytes 29427660 | solution.py:78
  6005.5 56.1 all-reduce.50.cloned.1.call-done
  6326.7 55.8 all-reduce.50.cloned.1.call-done
  6586.6 1252.7 %while.157 = (s32[]{:T(128)}, f32[768,384]{1,0:T(8,128)S(1)}, s32[]{:T(128)}, s32[]{:T(128)}, pred[]{:T(512)}, /*index=5*/s32[]{:T(128)}, s32[]{:T(128)}, s32[]{...) while((s32[]{:T(128)}, f32[768,384]{1,0:T(8,128)S(1)}, ...), condition=%wide.region_31.33_spmd.clone.clone, body=%wide.region_27.32_spmd.clone.clone.sunk | while | flops 227836112 | bytes 9078666 | solution.py:78
  7274.6 56.0 all-reduce.56.cloned.1.call-done
  7840.4 1246.2 %while.158 = (s32[]{:T(128)}, f32[512,256]{1,0:T(8,128)S(1)}, s32[]{:T(128)}, s32[]{:T(128)}, pred[]{:T(512)}, /*index=5*/s32[]{:T(128)}, s32[]{:T(128)}, s32[]{...) while((s32[]{:T(128)}, f32[512,256]{1,0:T(8,128)S(1)}, ...), condition=%wide.region_36.38_spmd.clone.clone, body=%wide.region_32.37_spmd.clone.clone.sunk | while | flops 135168192 | bytes 6031222 | solution.py:78
  9087.4 1062.8 %while.159 = (s32[]{:T(128)}, f32[256,128]{1,0:T(8,128)S(1)}, s32[]{:T(128)}, s32[]{:T(128)}, pred[]{:T(512)}, /*index=5*/s32[]{:T(128)}, s32[]{:T(128)}, s32[]{...) while((s32[]{:T(128)}, f32[256,128]{1,0:T(8,128)S(1)}, ...), condition=%wide.region_41.43_spmd.clone.clone, body=%wide.region_37.42_spmd.clone.clone.sunk | while | flops 59310264 | bytes 4033163 | solution.py:78
  (1719 shorter events, 8793.5 us)
Async XLA Ops:
  30.9 106.2 %all-reduce.26.cloned.1.call-start = ((), (), s32[]{:S(2)}) async-start(), calls=%async_computation.1 | async-start | bytes 1048576 | tf_op jit(solution)/shard_map/while/body/eval_jaxpr/psum | solution.py:67
  199.6 104.8 %all-reduce.26.cloned.1.call-start = ((), (), s32[]{:S(2)}) async-start(), calls=%async_computation.1 | async-start | bytes 1048576 | tf_op jit(solution)/shard_map/while/body/eval_jaxpr/psum | solution.py:67
  366.8 104.8 %all-reduce.26.cloned.1.call-start = ((), (), s32[]{:S(2)}) async-start(), calls=%async_computation.1 | async-start | bytes 1048576 | tf_op jit(solution)/shard_map/while/body/eval_jaxpr/psum | solution.py:67
  534.1 104.8 %all-reduce.26.cloned.1.call-start = ((), (), s32[]{:S(2)}) async-start(), calls=%async_computation.1 | async-start | bytes 1048576 | tf_op jit(solution)/shard_map/while/body/eval_jaxpr/psum | solution.py:67
  701.2 105.6 %all-reduce.26.cloned.1.call-start = ((), (), s32[]{:S(2)}) async-start(), calls=%async_computation.1 | async-start | bytes 1048576 | tf_op jit(solution)/shard_map/while/body/eval_jaxpr/psum | solution.py:67
  869.2 104.8 %all-reduce.26.cloned.1.call-start = ((), (), s32[]{:S(2)}) async-start(), calls=%async_computation.1 | async-start | bytes 1048576 | tf_op jit(solution)/shard_map/while/body/eval_jaxpr/psum | solution.py:67
  1036.4 105.4 %all-reduce.26.cloned.1.call-start = ((), (), s32[]{:S(2)}) async-start(), calls=%async_computation.1 | async-start | bytes 1048576 | tf_op jit(solution)/shard_map/while/body/eval_jaxpr/psum | solution.py:67
  1204.2 104.9 %all-reduce.26.cloned.1.call-start = ((), (), s32[]{:S(2)}) async-start(), calls=%async_computation.1 | async-start | bytes 1048576 | tf_op jit(solution)/shard_map/while/body/eval_jaxpr/psum | solution.py:67
  1377.8 104.6 %all-reduce.32.cloned.1.call-start = ((), (), s32[]{:S(2)}) async-start(), calls=%async_computation.4 | async-start | bytes 917504 | tf_op jit(solution)/shard_map/while/body/eval_jaxpr/psum | solution.py:67
  1543.2 104.6 %all-reduce.32.cloned.1.call-start = ((), (), s32[]{:S(2)}) async-start(), calls=%async_computation.4 | async-start | bytes 917504 | tf_op jit(solution)/shard_map/while/body/eval_jaxpr/psum | solution.py:67
  1708.6 104.6 %all-reduce.32.cloned.1.call-start = ((), (), s32[]{:S(2)}) async-start(), calls=%async_computation.4 | async-start | bytes 917504 | tf_op jit(solution)/shard_map/while/body/eval_jaxpr/psum | solution.py:67
  1874.0 104.6 %all-reduce.32.cloned.1.call-start = ((), (), s32[]{:S(2)}) async-start(), calls=%async_computation.4 | async-start | bytes 917504 | tf_op jit(solution)/shard_map/while/body/eval_jaxpr/psum | solution.py:67
  2039.4 105.4 %all-reduce.32.cloned.1.call-start = ((), (), s32[]{:S(2)}) async-start(), calls=%async_computation.4 | async-start | bytes 917504 | tf_op jit(solution)/shard_map/while/body/eval_jaxpr/psum | solution.py:67
  2205.7 104.6 %all-reduce.32.cloned.1.call-start = ((), (), s32[]{:S(2)}) async-start(), calls=%async_computation.4 | async-start | bytes 917504 | tf_op jit(solution)/shard_map/while/body/eval_jaxpr/psum | solution.py:67
  2371.2 105.1 %all-reduce.32.cloned.1.call-start = ((), (), s32[]{:S(2)}) async-start(), calls=%async_computation.4 | async-start | bytes 917504 | tf_op jit(solution)/shard_map/while/body/eval_jaxpr/psum | solution.py:67
  2537.2 104.6 %all-reduce.32.cloned.1.call-start = ((), (), s32[]{:S(2)}) async-start(), calls=%async_computation.4 | async-start | bytes 917504 | tf_op jit(solution)/shard_map/while/body/eval_jaxpr/psum | solution.py:67
  2713.8 104.2 %all-reduce.38.cloned.1.call-start = ((), (), s32[]{:S(2)}) async-start(), calls=%async_computation.7 | async-start | bytes 786432 | tf_op jit(solution)/shard_map/while/body/eval_jaxpr/psum | solution.py:67
  2877.5 104.2 %all-reduce.38.cloned.1.call-start = ((), (), s32[]{:S(2)}) async-start(), calls=%async_computation.7 | async-start | bytes 786432 | tf_op jit(solution)/shard_map/while/body/eval_jaxpr/psum | solution.py:67
  3041.3 104.2 %all-reduce.38.cloned.1.call-start = ((), (), s32[]{:S(2)}) async-start(), calls=%async_computation.7 | async-start | bytes 786432 | tf_op jit(solution)/shard_map/while/body/eval_jaxpr/psum | solution.py:67
  3205.1 104.2 %all-reduce.38.cloned.1.call-start = ((), (), s32[]{:S(2)}) async-start(), calls=%async_computation.7 | async-start | bytes 786432 | tf_op jit(solution)/shard_map/while/body/eval_jaxpr/psum | solution.py:67
  3369.0 105.1 %all-reduce.38.cloned.1.call-start = ((), (), s32[]{:S(2)}) async-start(), calls=%async_computation.7 | async-start | bytes 786432 | tf_op jit(solution)/shard_map/while/body/eval_jaxpr/psum | solution.py:67
  3533.5 104.2 %all-reduce.38.cloned.1.call-start = ((), (), s32[]{:S(2)}) async-start(), calls=%async_computation.7 | async-start | bytes 786432 | tf_op jit(solution)/shard_map/while/body/eval_jaxpr/psum | solution.py:67
  3697.2 104.8 %all-reduce.38.cloned.1.call-start = ((), (), s32[]{:S(2)}) async-start(), calls=%async_computation.7 | async-start | bytes 786432 | tf_op jit(solution)/shard_map/while/body/eval_jaxpr/psum | solution.py:67
  3861.6 104.2 %all-reduce.38.cloned.1.call-start = ((), (), s32[]{:S(2)}) async-start(), calls=%async_computation.7 | async-start | bytes 786432 | tf_op jit(solution)/shard_map/while/body/eval_jaxpr/psum | solution.py:67
  4030.9 106.0 %all-reduce.44.cloned.1.call-start = ((), (), s32[]{:S(2)}) async-start(), calls=%async_computation.10 | async-start | bytes 655360 | tf_op jit(solution)/shard_map/while/body/eval_jaxpr/psum | solution.py:67
  4190.9 105.9 %all-reduce.44.cloned.1.call-start = ((), (), s32[]{:S(2)}) async-start(), calls=%async_computation.10 | async-start | bytes 655360 | tf_op jit(solution)/shard_map/while/body/eval_jaxpr/psum | solution.py:67
  4350.8 105.9 %all-reduce.44.cloned.1.call-start = ((), (), s32[]{:S(2)}) async-start(), calls=%async_computation.10 | async-start | bytes 655360 | tf_op jit(solution)/shard_map/while/body/eval_jaxpr/psum | solution.py:67
  4510.7 105.9 %all-reduce.44.cloned.1.call-start = ((), (), s32[]{:S(2)}) async-start(), calls=%async_computation.10 | async-start | bytes 655360 | tf_op jit(solution)/shard_map/while/body/eval_jaxpr/psum | solution.py:67
  4670.5 106.7 %all-reduce.44.cloned.1.call-start = ((), (), s32[]{:S(2)}) async-start(), calls=%async_computation.10 | async-start | bytes 655360 | tf_op jit(solution)/shard_map/while/body/eval_jaxpr/psum | solution.py:67
  4831.0 105.9 %all-reduce.44.cloned.1.call-start = ((), (), s32[]{:S(2)}) async-start(), calls=%async_computation.10 | async-start | bytes 655360 | tf_op jit(solution)/shard_map/while/body/eval_jaxpr/psum | solution.py:67
  4990.9 106.5 %all-reduce.44.cloned.1.call-start = ((), (), s32[]{:S(2)}) async-start(), calls=%async_computation.10 | async-start | bytes 655360 | tf_op jit(solution)/shard_map/while/body/eval_jaxpr/psum | solution.py:67
  5151.2 105.9 %all-reduce.44.cloned.1.call-start = ((), (), s32[]{:S(2)}) async-start(), calls=%async_computation.10 | async-start | bytes 655360 | tf_op jit(solution)/shard_map/while/body/eval_jaxpr/psum | solution.py:67
  (169 other events, 12853.3 us)
Sparse Core Ops, SparseCore 0:
  81.1 55.9 all-reduce.25
  415.6 55.9 all-reduce.25
  582.9 55.9 all-reduce.25
  750.1 56.7 all-reduce.25
  918.0 55.9 all-reduce.25
  1085.2 56.5 all-reduce.25
  1253.0 56.0 all-reduce.25
  1426.4 55.8 all-reduce.31
  1757.2 55.8 all-reduce.31
  1922.6 55.8 all-reduce.31
  2088.0 56.7 all-reduce.31
  2254.3 55.8 all-reduce.31
  2419.9 56.4 all-reduce.31
  2585.8 55.8 all-reduce.31
  2762.2 55.7 all-reduce.37
  3089.8 55.7 all-reduce.37
  3253.6 55.7 all-reduce.37
  3417.4 56.5 all-reduce.37
  3582.0 55.7 all-reduce.37
  3745.6 56.2 all-reduce.37
  3910.1 55.7 all-reduce.37
  4081.3 55.5 all-reduce.43
  4401.2 55.4 all-reduce.43
  4720.9 56.2 all-reduce.43
  4881.5 55.4 all-reduce.43
  5041.4 55.9 all-reduce.43
  5201.7 55.4 all-reduce.43
  6005.6 56.0 all-reduce.49
  6326.7 55.7 all-reduce.49
  7274.7 55.9 all-reduce.55
  7588.3 55.6 all-reduce.55
  8524.8 55.6 all-reduce.61
  (152 shorter events, 6087.7 us)
where the time goes:
time: 10200 us
  waiting for transfers between devices  7860 us (77%)
  other arithmetic  1740 us (17%)
  matrix products  275 us (3%)
  local copies, waits for them, and re-layouts  149 us (1%)
  blocking collectives  107 us (1%)
    psum x64, waiting for transfers between devices, panel_step(): lax.psum(jnp.where(below_mask & own_col, solved_blocks, 0.0).astype(jnp.b...  3550 us
    psum x64, waiting for transfers between devices, panel_step(): diag_fac = lax.psum(jnp.where(is_owner, diag_own, 0.0), 'row')  2300 us
    psum x56, waiting for transfers between devices, transposed_panel(): return lax.psum(spread, 'row')  2000 us
    another operation x192, other arithmetic, panel_step(): jnp.linalg.cholesky(jnp.where(is_owner, diag_blk, eye_blk))  796 us
    another operation x128, other arithmetic, panel_step(): lax.linalg.triangular_solve(diag_fac, col_blk, left_side=False, lower=Tru...  636 us
    dot_general x64, matrix products, panel_step(): lax.dot_general(row_panel.reshape(win_rows, blk_size), col_panel.reshape(...  218 us
  transfers between devices with their start and end apart: 184, of which 184 were waited for; matrix products, arithmetic and copies ran while one was open for 1% of the time, Pallas kernels for 0%

commit v1 on v0

v1 whole, which is shorter than its diff:
```python
import functools
import jax
import jax.numpy as jnp
from jax import lax
from jax.experimental import pallas as pl
from jax.experimental.pallas import tpu as pltpu
from jax.sharding import PartitionSpec as P

MESH = pl.DeviceIdType.MESH
F32 = jnp.float32
BF16 = jnp.bfloat16
SUB = 8
NT = (((1,), (1,)), ((), ()))


def chol_inv(blk):
    n = blk.shape[0]
    lane = lax.broadcasted_iota(jnp.int32, (SUB, n), 1)
    sub = lax.broadcasted_iota(jnp.int32, (SUB, n), 0)
    t = blk
    lout = jnp.zeros((n, n), F32)
    l_rows, inv_rows = [], []
    for p in range(n // SUB):
        base = p * SUB
        rows = n - base
        more = rows > SUB
        cols = [jnp.broadcast_to(t[:, base + m:base + m + 1], (rows, n)) for m in range(SUB)]
        c0 = [c[:SUB] for c in cols]
        inside = (lane >= base) & (lane < base + SUB)
        t0 = jnp.where(inside, jnp.where(lane == sub + base, 1.0, 0.0), t[:SUB])
        o0 = lout[:SUB]
        if more:
            c1 = [c[SUB:] for c in cols]
            lane1 = lax.broadcasted_iota(jnp.int32, (rows - SUB, n), 1)
            t1 = jnp.where((lane1 >= base) & (lane1 < base + SUB), 0.0, t[SUB:])
            o1 = lout[SUB:]
        for j in range(SUB):
            r = lax.rsqrt(jnp.broadcast_to(c0[j][j:j + 1], (SUB, n)))
            l0 = c0[j] * r
            l0m = jnp.where(sub > j, l0, 0.0)
            urow = jnp.broadcast_to(t0[j:j + 1], (SUB, n)) * r
            o0 = jnp.where((lane == base + j) & (sub >= j), l0, o0)
            t0 = jnp.where(sub == j, urow, t0 - l0m * urow)
            spl = {m: jnp.broadcast_to(c0[m][j:j + 1], (SUB, n)) * r for m in range(j + 1, SUB)}
            for m in range(j + 1, SUB):
                c0[m] = c0[m] - l0m * spl[m]
            if more:
                reps = (rows - SUB) // SUB
                wide = lambda v: jnp.concatenate([v] * reps, axis=0) if reps > 1 else v
                l1 = c1[j] * wide(r)
                o1 = jnp.where(lane1 == base + j, l1, o1)
                t1 = t1 - l1 * wide(urow)
                for m in range(j + 1, SUB):
                    c1[m] = c1[m] - l1 * wide(spl[m])
        inv_rows.append(jnp.where(lane < base + SUB, t0, 0.0))
        l_rows.append(o0)
        if more:
            t, lout = t1, o1
    return jnp.concatenate(l_rows, axis=0), jnp.concatenate(inv_rows, axis=0)


def split3(x):
    hi = x.astype(BF16)
    rest = x - hi.astype(F32)
    mid = rest.astype(BF16)
    lo = (rest - mid.astype(F32)).astype(BF16)
    return hi, mid, lo


def inv_operands(linv):
    w1, w2, w3 = split3(linv)
    top = jnp.concatenate([w2, w1], axis=1)
    bot = jnp.concatenate([w1, w2], axis=1)
    return jnp.concatenate([top, bot, jnp.concatenate([w3, w1], axis=1)], axis=0)


def solve_f32(x, ops):
    n = x.shape[1]
    x1, x2, x3 = split3(x)
    main = lax.dot_general(jnp.concatenate([x1, x2], axis=1), ops[:2 * n], NT, preferred_element_type=F32)
    tail = lax.dot_general(jnp.concatenate([x1, x3], axis=1), ops[2 * n:], NT, preferred_element_type=F32)
    return (tail + main[:, :n]) + main[:, n:]


def gather_kernel(dims, a_ref, sd_ref, *rest):
    s, blk, row_devs, col_devs, nr, nc = dims
    wide = nc > 0
    if wide:
        rp_ref, up_ref, own_sd, own_rp, own_up, send, recv, loc = rest
    else:
        own_sd, send, recv, loc = rest
    per = col_devs // row_devs
    r = lax.axis_index("row")
    c = lax.axis_index("col")
    cores = 2
    ring_x = col_devs // cores
    x, core = c // cores, c % cores
    yp, ym, y2 = (r + 1) % row_devs, (r + row_devs - 1) % row_devs, (r + 2) % row_devs
    xp = ((x + 1) % ring_x) * cores + core
    xm = ((x + ring_x - 1) % ring_x) * cores + core
    x2 = ((x + 2) % ring_x) * cores + core
    par = x * cores + (1 - core)
    pxp, pxm, px2 = ((x + 1) % ring_x) * cores + 1 - core, ((x + ring_x - 1) % ring_x) * cores + 1 - core, ((x + 2) % ring_x) * cores + 1 - core

    h = per * blk
    row0, col0 = s * h, s * blk
    a_sd = a_ref.at[pl.ds(row0, h), pl.ds(col0, blk)]
    sd_in = pltpu.make_async_copy(a_sd, own_sd, loc.at[0])
    sd_in.start()
    if wide:
        a_rp = a_ref.at[pl.ds(row0 + h, nr * blk), pl.ds(col0, blk)]
        a_up = a_ref.at[pl.ds(row0, h), pl.ds(col0 + blk, nc * blk)]
        rp_in = pltpu.make_async_copy(a_rp, own_rp, loc.at[1])
        up_in = pltpu.make_async_copy(a_up, own_up, loc.at[2])
        rp_in.start()
        up_in.start()

    barrier = pltpu.get_barrier_semaphore()
    for row, col in ((yp, c), (ym, c), (r, xp), (r, xm), (r, par)):
        pl.semaphore_signal(barrier, inc=1, device_id={"row": row, "col": col}, device_id_type=MESH)
    pl.semaphore_wait(barrier, 5)

    sent = []

    def put(idx, src, dst, row, col):
        cp = pltpu.make_async_remote_copy(src_ref=src, dst_ref=dst, send_sem=send.at[idx], recv_sem=recv.at[idx],
                                          device_id={"row": row, "col": col}, device_id_type=MESH)
        cp.start()
        sent.append(cp)

    def got(idx, dst):
        pltpu.make_async_remote_copy(src_ref=dst, dst_ref=dst, send_sem=send.at[idx], recv_sem=recv.at[idx],
                                     device_id={"row": r, "col": c}, device_id_type=MESH).wait_recv()

    put(0, a_sd, sd_ref.at[c, r], yp, c)
    put(1, a_sd, sd_ref.at[c, r], ym, c)
    if wide:
        put(4, a_rp, rp_ref.at[c], r, xp)
        put(5, a_rp, rp_ref.at[c], r, xm)
        put(6, a_rp, rp_ref.at[c], r, par)
        put(13, a_up, up_ref.at[r], yp, c)
        put(14, a_up, up_ref.at[r], ym, c)
    sd_in.wait()
    sd_out = pltpu.make_async_copy(own_sd, sd_ref.at[c, r], loc.at[0])
    sd_out.start()
    if wide:
        rp_in.wait()
        rp_out = pltpu.make_async_copy(own_rp, rp_ref.at[c], loc.at[1])
        rp_out.start()
        up_in.wait()
        up_out = pltpu.make_async_copy(own_up, up_ref.at[r], loc.at[2])
        up_out.start()
    half_y = h // 2
    lo_y, hi_y = pl.ds(0, half_y), pl.ds(half_y, half_y)
    got(0, sd_ref.at[c, ym])
    put(2, sd_ref.at[c, ym, lo_y], sd_ref.at[c, ym, lo_y], yp, c)
    got(1, sd_ref.at[c, yp])
    put(3, sd_ref.at[c, yp, hi_y], sd_ref.at[c, yp, hi_y], ym, c)
    sd_out.wait()
    got(2, sd_ref.at[c, y2, lo_y])
    got(3, sd_ref.at[c, y2, hi_y])
    put(17, sd_ref.at[c], sd_ref.at[c], r, xp)
    put(18, sd_ref.at[c], sd_ref.at[c], r, xm)
    put(19, sd_ref.at[c], sd_ref.at[c], r, par)

    def ring_x_rest(first, ref, lo, hi):
        got(first, ref.at[xm])
        put(first + 3, ref.at[xm].at[lo], ref.at[xm].at[lo], r, xp)
        put(first + 5, ref.at[xm], ref.at[xm], r, par)
        got(first + 1, ref.at[xp])
        put(first + 4, ref.at[xp].at[hi], ref.at[xp].at[hi], r, xm)
        put(first + 6, ref.at[xp], ref.at[xp], r, par)

    def ring_x_end(first, ref, lo, hi):
        got(first + 3, ref.at[x2].at[lo])
        put(first + 7, ref.at[x2].at[lo], ref.at[x2].at[lo], r, par)
        got(first + 4, ref.at[x2].at[hi])
        put(first + 8, ref.at[x2].at[hi], ref.at[x2].at[hi], r, par)

    def ring_x_partner(first, ref, lo, hi):
        got(first + 2, ref.at[par])
        got(first + 5, ref.at[pxm])
        got(first + 6, ref.at[pxp])
        got(first + 7, ref.at[px2].at[lo])
        got(first + 8, ref.at[px2].at[hi])

    half_r = row_devs // 2
    sd_halves = (pl.ds(0, half_r), pl.ds(half_r, half_r))
    if wide:
        half_p = nr * blk // 2
        rp_halves = (pl.ds(0, half_p), pl.ds(half_p, half_p))
        ring_x_rest(4, rp_ref, *rp_halves)
        got(13, up_ref.at[ym])
        put(15, up_ref.at[ym, lo_y], up_ref.at[ym, lo_y], yp, c)
        got(14, up_ref.at[yp])
        put(16, up_ref.at[yp, hi_y], up_ref.at[yp, hi_y], ym, c)
    ring_x_rest(17, sd_ref, *sd_halves)
    if wide:
        ring_x_end(4, rp_ref, *rp_halves)
    ring_x_end(17, sd_ref, *sd_halves)
    if wide:
        got(15, up_ref.at[y2, lo_y])
        got(16, up_ref.at[y2, hi_y])
        ring_x_partner(4, rp_ref, *rp_halves)
        rp_out.wait()
        up_out.wait()
    ring_x_partner(17, sd_ref, *sd_halves)
    for cp in sent:
        cp.wait_send()


def gather(a2, s, blk, row_devs, col_devs, nr, nc):
    per = col_devs // row_devs
    h = per * blk
    outs = [jax.ShapeDtypeStruct((col_devs, row_devs, h, blk), F32)]
    scratch = [pltpu.VMEM((h, blk), F32)]
    if nc:
        outs += [jax.ShapeDtypeStruct((col_devs, nr * blk, blk), F32), jax.ShapeDtypeStruct((row_devs, h, nc * blk), F32)]
        scratch += [pltpu.VMEM((nr * blk, blk), F32), pltpu.VMEM((h, nc * blk), F32)]
    anyspec = pl.BlockSpec(memory_space=pl.ANY)
    return pl.pallas_call(
        functools.partial(gather_kernel, (s, blk, row_devs, col_devs, nr, nc)),
        out_shape=outs,
        in_specs=[anyspec],
        out_specs=[anyspec] * len(outs),
        scratch_shapes=scratch + [pltpu.SemaphoreType.DMA((26,)), pltpu.SemaphoreType.DMA((26,)), pltpu.SemaphoreType.DMA((3,))],
        compiler_params=pltpu.CompilerParams(collective_id=s, has_side_effects=True),
        name=f"gather_{s}",
    )(a2)


def factor_kernel(dims, a_ref, sd_hbm, *rest):
    s, blk, row_devs, col_devs, nr, nc = dims
    wide = nc > 0
    if wide:
        rp_hbm, up_hbm, out_ref, sd, dblk, linv, bsd, zero, sems, pan, up, w, bpan = rest
    else:
        out_ref, sd, dblk, linv, bsd, zero, sems = rest
    per = col_devs // row_devs
    h = per * blk
    row0, col0 = s * h, s * blk
    r = lax.axis_index("row")
    c = lax.axis_index("col")
    sd_in = pltpu.make_async_copy(sd_hbm, sd, sems.at[0])
    sd_in.start()
    if wide:
        up_in = pltpu.make_async_copy(up_hbm, up, sems.at[2])
        up_in.start()
        rp_in = pltpu.make_async_copy(rp_hbm, pan.at[:, pl.ds(0, nr * blk)], sems.at[1])
        rp_in.start()
        w_in = pltpu.make_async_copy(a_ref.at[pl.ds(row0 + h, nr * blk), pl.ds(col0 + blk, nc * blk)], w, sems.at[3])
        w_in.start()
        zero[...] = jnp.zeros_like(zero)
        z_out = pltpu.make_async_copy(zero, out_ref.at[pl.ds(row0, h), pl.ds(col0 + blk, nc * blk)], sems.at[4])
        z_out.start()
    sd_in.wait()

    def at(j, k):
        return (k, j % row_devs, pl.ds((j // row_devs) * blk, blk))

    dblk[...] = sd[at(0, 0)]

    @pl.loop(0, col_devs)
    def _(k):
        lfac, inv = chol_inv(dblk[...])
        dblk[...] = lfac
        linv[k] = inv_operands(inv)
        for kk in range(col_devs):
            @pl.when(k == kk)
            def _():
                sd[at(kk, kk)] = dblk[...]
                if kk + 1 < col_devs:
                    ops = linv[kk]
                    below = jnp.concatenate([sd[at(j, kk)] for j in range(kk + 1, col_devs)], axis=0)
                    low = solve_f32(below, ops)
                    for j in range(kk + 1, col_devs):
                        sd[at(j, kk)] = low[(j - kk - 1) * blk:(j - kk) * blk]
                    bsd[(kk + 1) * blk:, kk * blk:(kk + 1) * blk] = low.astype(BF16)
                    upd = lax.dot_general(bsd[(kk + 1) * blk:, :(kk + 1) * blk], bsd[(kk + 1) * blk:(kk + 2) * blk, :(kk + 1) * blk], NT,
                                          preferred_element_type=F32)
                    dblk[...] = sd[at(kk + 1, kk + 1)] - upd[:blk]
                    for j in range(kk + 2, col_devs):
                        sd[at(j, kk + 1)] = sd[at(j, kk + 1)] - upd[(j - kk - 1) * blk:(j - kk) * blk]

    for tt in range(per):
        own = sd[c, r, pl.ds(tt * blk, blk)]
        sd[c, r, pl.ds(tt * blk, blk)] = jnp.where(tt * row_devs + r >= c, own, jnp.zeros_like(own))
    d_out = pltpu.make_async_copy(sd.at[c, r], out_ref.at[pl.ds(row0, h), pl.ds(col0, blk)], sems.at[0])
    d_out.start()
    if wide:
        up_in.wait()
        rp_in.wait()
        for k in range(col_devs):
            for jj in range(nc):
                pan[k, pl.ds((nr + jj) * blk, blk)] = up[k % row_devs, pl.ds((k // row_devs) * blk, blk), pl.ds(jj * blk, blk)].T
        for k in range(col_devs):
            ops = linv[k]

            @pl.loop(0, nr + nc)
            def _(i):
                sl = pl.ds(pl.multiple_of(i * blk, blk), blk)
                cur = pan[k, sl]
                if k:
                    cur = cur - lax.dot_general(bpan[sl, :k * blk], bsd[k * blk:(k + 1) * blk, :k * blk], NT, preferred_element_type=F32)
                low = solve_f32(cur, ops)
                pan[k, sl] = low
                bpan[sl, k * blk:(k + 1) * blk] = low.astype(BF16)
        l_out = pltpu.make_async_copy(pan.at[c, pl.ds(0, nr * blk)], out_ref.at[pl.ds(row0 + h, nr * blk), pl.ds(col0, blk)], sems.at[1])
        l_out.start()
        w_in.wait()

        @pl.loop(0, nr // 2)
        def _(i):
            sl = pl.ds(pl.multiple_of(i * 2 * blk, 2 * blk), 2 * blk)
            w[sl] = w[sl] - lax.dot_general(bpan[sl], bpan[nr * blk:], NT, preferred_element_type=F32)
        w_out = pltpu.make_async_copy(w, out_ref.at[pl.ds(row0 + h, nr * blk), pl.ds(col0 + blk, nc * blk)], sems.at[3])
        w_out.start()
        w_out.wait()
        l_out.wait()
        z_out.wait()
    d_out.wait()


def factor(a2, parts, s, blk, row_devs, col_devs, nr, nc):
    per = col_devs // row_devs
    h = per * blk
    anyspec = pl.BlockSpec(memory_space=pl.ANY)
    scratch = [
        pltpu.VMEM((col_devs, row_devs, h, blk), F32),
        pltpu.VMEM((blk, blk), F32),
        pltpu.VMEM((col_devs, 3 * blk, 2 * blk), BF16),
        pltpu.VMEM((col_devs * blk, col_devs * blk), BF16),
        pltpu.VMEM((h, max(nc, 1) * blk), F32),
        pltpu.SemaphoreType.DMA((5,)),
    ]
    if nc:
        scratch += [
            pltpu.VMEM((col_devs, (nr + nc) * blk, blk), F32),
            pltpu.VMEM((row_devs, h, nc * blk), F32),
            pltpu.VMEM((nr * blk, nc * blk), F32),
            pltpu.VMEM(((nr + nc) * blk, col_devs * blk), BF16),
        ]
    return pl.pallas_call(
        functools.partial(factor_kernel, (s, blk, row_devs, col_devs, nr, nc)),
        out_shape=jax.ShapeDtypeStruct(a2.shape, F32),
        in_specs=[anyspec] * (1 + len(parts)),
        out_specs=anyspec,
        scratch_shapes=scratch,
        input_output_aliases={} if s == 0 else {0: 0},
        compiler_params=pltpu.CompilerParams(vmem_limit_bytes=60 * 1024 * 1024),
        name=f"factor_{s}",
    )(a2, *parts)


def solution(mesh):
    row_devs = mesh.shape["row"]
    col_devs = mesh.shape["col"]
    per = col_devs // row_devs

    def factor_local(a_loc):
        row_blocks, blk, local_cols = a_loc.shape
        col_blocks = local_cols // blk
        a2 = a_loc.reshape(row_blocks * blk, local_cols)
        for s in range(col_blocks):
            nr, nc = row_blocks - per * (s + 1), col_blocks - s - 1
            parts = gather(a2, s, blk, row_devs, col_devs, nr, nc)
            a2 = factor(a2, parts, s, blk, row_devs, col_devs, nr, nc)
        return a2.reshape(row_blocks, blk, local_cols)

    spec = P(("batch", "row"), None, "col")
    return jax.shard_map(factor_local, mesh=mesh, in_specs=(spec,), out_specs=spec, check_vma=False)
```

time: 10200 us -> 938 us (0.09)
  waiting for transfers between devices: 7860 us -> 0 us
  other arithmetic: 1740 us -> 0 us
  Pallas kernels: 0 us -> 931 us
  matrix products: 275 us -> 0 us
  local copies, waits for them, and re-layouts: 149 us -> 0 us
  blocking collectives: 107 us -> 0 us
    psum x184 -> x0, waiting for transfers between devices: 7850 us -> none  [the longest x64 3550 us: panel_step(): lax.psum(jnp.where(below_mask & own_col, solved_blocks, 0.0).astype(jnp.b...]
    another operation x320 -> x0, other arithmetic: 1430 us -> none  [the longest x192 796 us: panel_step(): jnp.linalg.cholesky(jnp.where(is_owner, diag_blk, eye_blk))]
    pallas_call x0 -> x16, Pallas kernels: none -> 931 us  [the longest x8 572 us: factor(): pl.pallas_call(functools.partial(factor_kernel, (s, blk, row_devs, col_de...]
    dot_general x64 -> x0, matrix products: 218 us -> none  [panel_step(): lax.dot_general(row_panel.reshape(win_rows, blk_size), col_panel.reshape(...]
    select_n x185 -> x0, other arithmetic: 213 us -> none  [the longest x56 89.1 us: transposed_panel(): jnp.where(row_id == col_id % row_devs, chosen, jnp.zeros_like(chosen))]
    psum x8 -> x0, blocking collectives: 107 us -> none  [transposed_panel(): return lax.psum(spread, 'row')]
  transfers between devices with their start and end apart: 184 -> 0, of which waited for: 184 -> 0; matrix products, arithmetic and copies ran while one was open for 1% -> 0% of each run, Pallas kernels for 0% -> 0%
where the time goes in v1:
time: 938 us; the launch traced here: 931 us
  Pallas kernels  931 us (99%)
    pallas_call x8, Pallas kernels, factor(): pl.pallas_call(functools.partial(factor_kernel, (s, blk, row_devs, col_de...  572 us
    pallas_call x8, Pallas kernels, gather(): pl.pallas_call(functools.partial(gather_kernel, (s, blk, row_devs, col_de...  359 us

profile of v1, /device:TPU:97, one launch (start us, length us, event | category | flops | bytes accessed | tf_op | source)
XLA Modules:
  0.0 931.0 jit_solution(17773303508008842956)
XLA Ops:
  0.0 63.2 %gather_0.1 = (f32[8,4,256,128]{3,2,1,0:T(8,128)}, f32[8,1792,128]{2,1,0:T(8,128)}, f32[4,256,896]{2,1,0:T(8,128)}) custom-call(f32[2048,1024]{1,0:T(8,128)} %bitcast.2), custom_call_target="tpu_custom_call" | custom-call | tf_op jit(solution)/shard_map/gather_0/pallas_call | solution.py:221
  63.2 105.1 %factor_0.1.a_ref = f32[2048,1024]{1,0:T(8,128)} custom-call(f32[2048,1024]{1,0:T(8,128)} %bitcast.3, f32[8,4,256,128]{3,2,1,0:T(8,128)} %get-tuple-element.26.sd_hbm, f32[8,1792,128]{2,1,0:T(8,128)} %get-tuple-element.27.rest_0_, f32[4,256,896]{2,1,0:T(8,128)} %get-tuple-element.28.rest_1_), custom_call_target="tpu_custom_call" | custom-call | tf_op jit(solution)/shard_map/factor_0/pallas_call | solution.py:343
  168.4 55.3 %gather_1.1 = (f32[8,4,256,128]{3,2,1,0:T(8,128)}, f32[8,1536,128]{2,1,0:T(8,128)}, f32[4,256,768]{2,1,0:T(8,128)}) custom-call(f32[2048,1024]{1,0:T(8,128)} %factor_0.1.a_ref), custom_call_target="tpu_custom_call" | custom-call | tf_op jit(solution)/shard_map/gather_1/pallas_call | solution.py:221
  223.7 94.9 %factor_1.1.a_ref = f32[2048,1024]{1,0:T(8,128)} custom-call(f32[2048,1024]{1,0:T(8,128)} %factor_0.1.a_ref, f32[8,4,256,128]{3,2,1,0:T(8,128)} %get-tuple-element.29.sd_hbm, f32[8,1536,128]{2,1,0:T(8,128)} %get-tuple-element.30.rest_0_, f32[4,256,768]{2,1,0:T(8,128)} %get-tuple-element.31.rest_1_), custom_call_target="tpu_custom_call", output_to_operand_aliasing={{}: (0, {})} | custom-call | tf_op jit(solution)/shard_map/factor_1/pallas_call | solution.py:343
  318.6 50.0 %gather_2.1 = (f32[8,4,256,128]{3,2,1,0:T(8,128)}, f32[8,1280,128]{2,1,0:T(8,128)}, f32[4,256,640]{2,1,0:T(8,128)}) custom-call(f32[2048,1024]{1,0:T(8,128)} %factor_1.1.a_ref), custom_call_target="tpu_custom_call" | custom-call | tf_op jit(solution)/shard_map/gather_2/pallas_call | solution.py:221
  368.6 85.7 %factor_2.1.a_ref = f32[2048,1024]{1,0:T(8,128)} custom-call(f32[2048,1024]{1,0:T(8,128)} %factor_1.1.a_ref, f32[8,4,256,128]{3,2,1,0:T(8,128)} %get-tuple-element.32.sd_hbm, f32[8,1280,128]{2,1,0:T(8,128)} %get-tuple-element.33.rest_0_, f32[4,256,640]{2,1,0:T(8,128)} %get-tuple-element.34.rest_1_), custom_call_target="tpu_custom_call", output_to_operand_aliasing={{}: (0, {})} | custom-call | tf_op jit(solution)/shard_map/factor_2/pallas_call | solution.py:343
  454.3 46.8 %gather_3.1 = (f32[8,4,256,128]{3,2,1,0:T(8,128)}, f32[8,1024,128]{2,1,0:T(8,128)}, f32[4,256,512]{2,1,0:T(8,128)}) custom-call(f32[2048,1024]{1,0:T(8,128)} %factor_2.1.a_ref), custom_call_target="tpu_custom_call" | custom-call | tf_op jit(solution)/shard_map/gather_3/pallas_call | solution.py:221
  501.2 75.4 %factor_3.1.a_ref = f32[2048,1024]{1,0:T(8,128)} custom-call(f32[2048,1024]{1,0:T(8,128)} %factor_2.1.a_ref, f32[8,4,256,128]{3,2,1,0:T(8,128)} %get-tuple-element.35.sd_hbm, f32[8,1024,128]{2,1,0:T(8,128)} %get-tuple-element.36.rest_0_, f32[4,256,512]{2,1,0:T(8,128)} %get-tuple-element.37.rest_1_), custom_call_target="tpu_custom_call", output_to_operand_aliasing={{}: (0, {})} | custom-call | tf_op jit(solution)/shard_map/factor_3/pallas_call | solution.py:343
  576.6 41.5 %gather_4.1 = (f32[8,4,256,128]{3,2,1,0:T(8,128)}, f32[8,768,128]{2,1,0:T(8,128)}, f32[4,256,384]{2,1,0:T(8,128)}) custom-call(f32[2048,1024]{1,0:T(8,128)} %factor_3.1.a_ref), custom_call_target="tpu_custom_call" | custom-call | tf_op jit(solution)/shard_map/gather_4/pallas_call | solution.py:221
  618.2 66.3 %factor_4.1.a_ref = f32[2048,1024]{1,0:T(8,128)} custom-call(f32[2048,1024]{1,0:T(8,128)} %factor_3.1.a_ref, f32[8,4,256,128]{3,2,1,0:T(8,128)} %get-tuple-element.38.sd_hbm, f32[8,768,128]{2,1,0:T(8,128)} %get-tuple-element.39.rest_0_, f32[4,256,384]{2,1,0:T(8,128)} %get-tuple-element.40.rest_1_), custom_call_target="tpu_custom_call", output_to_operand_aliasing={{}: (0, {})} | custom-call | tf_op jit(solution)/shard_map/factor_4/pallas_call | solution.py:343
  684.4 38.4 %gather_5.1 = (f32[8,4,256,128]{3,2,1,0:T(8,128)}, f32[8,512,128]{2,1,0:T(8,128)}, f32[4,256,256]{2,1,0:T(8,128)}) custom-call(f32[2048,1024]{1,0:T(8,128)} %factor_4.1.a_ref), custom_call_target="tpu_custom_call" | custom-call | tf_op jit(solution)/shard_map/gather_5/pallas_call | solution.py:221
  722.9 57.0 %factor_5.1.a_ref = f32[2048,1024]{1,0:T(8,128)} custom-call(f32[2048,1024]{1,0:T(8,128)} %factor_4.1.a_ref, f32[8,4,256,128]{3,2,1,0:T(8,128)} %get-tuple-element.41.sd_hbm, f32[8,512,128]{2,1,0:T(8,128)} %get-tuple-element.42.rest_0_, f32[4,256,256]{2,1,0:T(8,128)} %get-tuple-element.43.rest_1_), custom_call_target="tpu_custom_call", output_to_operand_aliasing={{}: (0, {})} | custom-call | tf_op jit(solution)/shard_map/factor_5/pallas_call | solution.py:343
  779.9 33.1 %gather_6.1 = (f32[8,4,256,128]{3,2,1,0:T(8,128)}, f32[8,256,128]{2,1,0:T(8,128)}, f32[4,256,128]{2,1,0:T(8,128)}) custom-call(f32[2048,1024]{1,0:T(8,128)} %factor_5.1.a_ref), custom_call_target="tpu_custom_call" | custom-call | tf_op jit(solution)/shard_map/gather_6/pallas_call | solution.py:221
  813.0 48.3 %factor_6.1.a_ref = f32[2048,1024]{1,0:T(8,128)} custom-call(f32[2048,1024]{1,0:T(8,128)} %factor_5.1.a_ref, f32[8,4,256,128]{3,2,1,0:T(8,128)} %get-tuple-element.44.sd_hbm, f32[8,256,128]{2,1,0:T(8,128)} %get-tuple-element.45.rest_0_, f32[4,256,128]{2,1,0:T(8,128)} %get-tuple-element.46.rest_1_), custom_call_target="tpu_custom_call", output_to_operand_aliasing={{}: (0, {})} | custom-call | tf_op jit(solution)/shard_map/factor_6/pallas_call | solution.py:343
  861.4 30.1 %gather_7.1.sd_hbm = f32[8,4,256,128]{3,2,1,0:T(8,128)} custom-call(f32[2048,1024]{1,0:T(8,128)} %factor_6.1.a_ref), custom_call_target="tpu_custom_call" | custom-call | tf_op jit(solution)/shard_map/gather_7/pallas_call | solution.py:221
  891.5 39.3 %factor_7.1 = f32[2048,1024]{1,0:T(8,128)} custom-call(f32[2048,1024]{1,0:T(8,128)} %factor_6.1.a_ref, f32[8,4,256,128]{3,2,1,0:T(8,128)} %gather_7.1.sd_hbm), custom_call_target="tpu_custom_call", output_to_operand_aliasing={{}: (0, {})} | custom-call | tf_op jit(solution)/shard_map/factor_7/pallas_call | solution.py:343

commit v2 on v1

--- a/solution.py
+++ b/solution.py
@@ -229,35 +229,22 @@
     )(a2)
 
 
-def factor_kernel(dims, a_ref, sd_hbm, *rest):
-    s, blk, row_devs, col_devs, nr, nc = dims
-    wide = nc > 0
-    if wide:
-        rp_hbm, up_hbm, out_ref, sd, dblk, linv, bsd, zero, sems, pan, up, w, bpan = rest
-    else:
-        out_ref, sd, dblk, linv, bsd, zero, sems = rest
-    per = col_devs // row_devs
-    h = per * blk
-    row0, col0 = s * h, s * blk
+def last_kernel(dims, a_ref, sd_hbm, out_ref, sd, dblk, linv, bsd, whole, sdsem, loc):
+    s, blk, row_devs, col_devs = dims
+    h = (col_devs // row_devs) * blk
     r = lax.axis_index("row")
     c = lax.axis_index("col")
-    sd_in = pltpu.make_async_copy(sd_hbm, sd, sems.at[0])
-    sd_in.start()
-    if wide:
-        up_in = pltpu.make_async_copy(up_hbm, up, sems.at[2])
-        up_in.start()
-        rp_in = pltpu.make_async_copy(rp_hbm, pan.at[:, pl.ds(0, nr * blk)], sems.at[1])
-        rp_in.start()
-        w_in = pltpu.make_async_copy(a_ref.at[pl.ds(row0 + h, nr * blk), pl.ds(col0 + blk, nc * blk)], w, sems.at[3])
-        w_in.start()
-        zero[...] = jnp.zeros_like(zero)
-        z_out = pltpu.make_async_copy(zero, out_ref.at[pl.ds(row0, h), pl.ds(col0 + blk, nc * blk)], sems.at[4])
-        z_out.start()
-    sd_in.wait()
+    sd_in = [pltpu.make_async_copy(sd_hbm.at[k], sd.at[k], sdsem.at[k]) for k in range(col_devs)]
+    for cp in sd_in:
+        cp.start()
+    a_in = pltpu.make_async_copy(a_ref, whole, loc.at[0])
+    a_in.start()
+    a_out = pltpu.make_async_copy(whole, out_ref, loc.at[1])
 
     def at(j, k):
         return (k, j % row_devs, pl.ds((j // row_devs) * blk, blk))
 
+    sd_in[0].wait()
     dblk[...] = sd[at(0, 0)]
 
     @pl.loop(0, col_devs)
@@ -268,88 +255,302 @@
         for kk in range(col_devs):
             @pl.when(k == kk)
             def _():
-                sd[at(kk, kk)] = dblk[...]
-                if kk + 1 < col_devs:
-                    ops = linv[kk]
-                    below = jnp.concatenate([sd[at(j, kk)] for j in range(kk + 1, col_devs)], axis=0)
-                    low = solve_f32(below, ops)
-                    for j in range(kk + 1, col_devs):
-                        sd[at(j, kk)] = low[(j - kk - 1) * blk:(j - kk) * blk]
-                    bsd[(kk + 1) * blk:, kk * blk:(kk + 1) * blk] = low.astype(BF16)
-                    upd = lax.dot_general(bsd[(kk + 1) * blk:, :(kk + 1) * blk], bsd[(kk + 1) * blk:(kk + 2) * blk, :(kk + 1) * blk], NT,
-                                          preferred_element_type=F32)
-                    dblk[...] = sd[at(kk + 1, kk + 1)] - upd[:blk]
-                    for j in range(kk + 2, col_devs):
-                        sd[at(j, kk + 1)] = sd[at(j, kk + 1)] - upd[(j - kk - 1) * blk:(j - kk) * blk]
-
-    for tt in range(per):
-        own = sd[c, r, pl.ds(tt * blk, blk)]
-        sd[c, r, pl.ds(tt * blk, blk)] = jnp.where(tt * row_devs + r >= c, own, jnp.zeros_like(own))
-    d_out = pltpu.make_async_copy(sd.at[c, r], out_ref.at[pl.ds(row0, h), pl.ds(col0, blk)], sems.at[0])
+                chain_rest(kk, at, sd_in, sd, dblk, linv, bsd, blk, col_devs)
+                if kk == col_devs // 2:
+                    a_in.wait()
+                    a_out.start()
+
+    for tt in range(col_devs // row_devs):
+        val = sd[c, r, pl.ds(tt * blk, blk)]
+        sd[c, r, pl.ds(tt * blk, blk)] = jnp.where(tt * row_devs + r >= c, val, jnp.zeros_like(val))
+    a_out.wait()
+    d_out = pltpu.make_async_copy(sd.at[c, r], out_ref.at[s, :, pl.ds(s * blk, blk)], loc.at[0])
     d_out.start()
-    if wide:
-        up_in.wait()
-        rp_in.wait()
-        for k in range(col_devs):
-            for jj in range(nc):
-                pan[k, pl.ds((nr + jj) * blk, blk)] = up[k % row_devs, pl.ds((k // row_devs) * blk, blk), pl.ds(jj * blk, blk)].T
+    d_out.wait()
+
+
+def last(a3, sd, s, blk, row_devs, col_devs):
+    anyspec = pl.BlockSpec(memory_space=pl.ANY)
+    h = (col_devs // row_devs) * blk
+    return pl.pallas_call(
+        functools.partial(last_kernel, (s, blk, row_devs, col_devs)),
+        out_shape=jax.ShapeDtypeStruct(a3.shape, F32),
+        in_specs=[anyspec, anyspec],
+        out_specs=anyspec,
+        scratch_shapes=[
+            pltpu.VMEM((col_devs, row_devs, h, blk), F32),
+            pltpu.VMEM((blk, blk), F32),
+            pltpu.VMEM((col_devs, 3 * blk, 2 * blk), BF16),
+            pltpu.VMEM((col_devs * blk, col_devs * blk), BF16),
+            pltpu.VMEM(a3.shape, F32),
+            pltpu.SemaphoreType.DMA((col_devs,)),
+            pltpu.SemaphoreType.DMA((2,)),
+        ],
+        compiler_params=pltpu.CompilerParams(vmem_limit_bytes=60 * 1024 * 1024),
+        name=f"last_{s}",
+    )(a3, sd)
+
+
+def chain_rest(kk, at, sd_in, sd, dblk, linv, bsd, blk, col_devs):
+    sd[at(kk, kk)] = dblk[...]
+    if kk + 1 < col_devs:
+        sd_in[kk + 1].wait()
+        below = jnp.concatenate([sd[at(j, kk)] for j in range(kk + 1, col_devs)], axis=0)
+        low = solve_f32(below, linv[kk])
+        for j in range(kk + 1, col_devs):
+            sd[at(j, kk)] = low[(j - kk - 1) * blk:(j - kk) * blk]
+        bsd[(kk + 1) * blk:, kk * blk:(kk + 1) * blk] = low.astype(BF16)
+        upd = lax.dot_general(bsd[(kk + 1) * blk:, :(kk + 1) * blk], bsd[(kk + 1) * blk:(kk + 2) * blk, :(kk + 1) * blk], NT,
+                              preferred_element_type=F32)
+        dblk[...] = sd[at(kk + 1, kk + 1)] - upd[:blk]
+        for j in range(kk + 2, col_devs):
+            sd[at(j, kk + 1)] = sd[at(j, kk + 1)] - upd[(j - kk - 1) * blk:(j - kk) * blk]
+
+
+def fused_kernel(dims, a_ref, sd_hbm, out_ref, sdn, sd, dblk, linv, bsd, zero, pan, up, w, bi, bj, bq, own, send, recv, loc, sdsem):
+    s, blk, row_devs, col_devs, nq = dims
+    h = (col_devs // row_devs) * blk
+    r = lax.axis_index("row")
+    c = lax.axis_index("col")
+    cores = 2
+    ring = col_devs // cores
+    x, core = c // cores, c % cores
+    yp, ym, y2 = (r + 1) % row_devs, (r + row_devs - 1) % row_devs, (r + 2) % row_devs
+    ix = lambda d, k: ((x + d) % ring) * cores + k
+    xp, xm, x2, par = ix(1, core), ix(ring - 1, core), ix(2, core), ix(0, 1 - core)
+    pxp, pxm, px2 = ix(1, 1 - core), ix(ring - 1, 1 - core), ix(2, 1 - core)
+    lanes = pl.ds(s * blk, blk)
+    right = pl.ds((s + 1) * blk, nq * blk)
+    under = pl.ds(s + 1, nq)
+    a_rp, a_up = a_ref.at[under, :, lanes], a_ref.at[s, :, right]
+    top, bot, both = pl.ds(0, blk), pl.ds(blk, blk), pl.ds(0, h)
+    half = row_devs // 2
+    lo, hi = pl.ds(0, half), pl.ds(half, half)
+    table = {}
+
+    def add(name, src, dst, row, col, arrive):
+        table[name] = (len(table), src, dst, row, col, arrive)
+
+    add("up+", a_up, up.at[r], yp, c, up.at[ym])
+    add("up-", a_up, up.at[r], ym, c, up.at[yp])
+    add("upf+", up.at[ym, top], up.at[ym, top], yp, c, up.at[y2, top])
+    add("upf-", up.at[yp, bot], up.at[yp, bot], ym, c, up.at[y2, bot])
+    rows = lambda i, part: pan.at[i, :, part]
+    add("rp+", a_rp, rows(c, both), r, xp, rows(xm, both))
+    add("rp-", a_rp, rows(c, both), r, xm, rows(xp, both))
+    add("rpp", a_rp, rows(c, both), r, par, rows(par, both))
+    add("rpf+", rows(xm, top), rows(xm, top), r, xp, rows(x2, top))
+    add("rpf-", rows(xp, bot), rows(xp, bot), r, xm, rows(x2, bot))
+    add("rpr1", rows(xm, both), rows(xm, both), r, par, rows(pxm, both))
+    add("rpr2", rows(xp, both), rows(xp, both), r, par, rows(pxp, both))
+    add("rpr3", rows(x2, top), rows(x2, top), r, par, rows(px2, top))
+    add("rpr4", rows(x2, bot), rows(x2, bot), r, par, rows(px2, bot))
+    add("sy+", sdn.at[c, r], sdn.at[c, r], yp, c, sdn.at[c, ym])
+    add("sy-", sdn.at[c, r], sdn.at[c, r], ym, c, sdn.at[c, yp])
+    add("syf+", sdn.at[c, ym, top], sdn.at[c, ym, top], yp, c, sdn.at[c, y2, top])
+    add("syf-", sdn.at[c, yp, bot], sdn.at[c, yp, bot], ym, c, sdn.at[c, y2, bot])
+    for tag, part in (("lo", lo), ("hi", hi)):
+        add("sx+" + tag, sdn.at[c, part], sdn.at[c, part], r, xp, sdn.at[xm, part])
+        add("sx-" + tag, sdn.at[c, part], sdn.at[c, part], r, xm, sdn.at[xp, part])
+        add("sr1" + tag, sdn.at[xm, part], sdn.at[xm, part], r, par, sdn.at[pxm, part])
+        add("sr2" + tag, sdn.at[xp, part], sdn.at[xp, part], r, par, sdn.at[pxp, part])
+        add("sr3" + tag, sdn.at[x2, part], sdn.at[x2, part], r, par, sdn.at[px2, part])
+    add("sxp", sdn.at[c], sdn.at[c], r, par, sdn.at[par])
+    add("sxf+", sdn.at[xm, lo], sdn.at[xm, lo], r, xp, sdn.at[x2, lo])
+    add("sxf-", sdn.at[xp, hi], sdn.at[xp, hi], r, xm, sdn.at[x2, hi])
+
+    def remote(name):
+        idx, src, dst, row, col, _ = table[name]
+        return pltpu.make_async_remote_copy(src_ref=src, dst_ref=dst, send_sem=send.at[idx], recv_sem=recv.at[idx],
+                                            device_id={"row": row, "col": col}, device_id_type=MESH)
+
+    def start(*names):
+        for name in names:
+            remote(name).start()
+
+    def got(*names):
+        for name in names:
+            idx, arrive = table[name][0], table[name][5]
+            pltpu.make_async_remote_copy(src_ref=arrive, dst_ref=arrive, send_sem=send.at[idx], recv_sem=recv.at[idx],
+                                         device_id={"row": r, "col": c}, device_id_type=MESH).wait_recv()
+
+    def gone(*names):
+        for name in names:
+            remote(name).wait_send()
+
+    sd_in = [pltpu.make_async_copy(sd_hbm.at[k], sd.at[k], sdsem.at[k]) for k in range(col_devs)]
+    for cp in sd_in:
+        cp.start()
+    rp_in = pltpu.make_async_copy(a_rp, rows(c, both), loc.at[0])
+    up_in = pltpu.make_async_copy(a_up, up.at[r], loc.at[1])
+    w_in = pltpu.make_async_copy(a_ref.at[under, :, right], w, loc.at[2])
+    z_out = pltpu.make_async_copy(zero, out_ref.at[s, :, right], loc.at[3])
+    d_out = pltpu.make_async_copy(sd.at[c, r], out_ref.at[s, :, lanes], loc.at[4])
+    l_out = pltpu.make_async_copy(rows(c, both), out_ref.at[under, :, lanes], loc.at[5])
+    n_out = pltpu.make_async_copy(own, sdn.at[c, r], loc.at[6])
+    w_out = pltpu.make_async_copy(w, out_ref.at[under, :, right], loc.at[7])
+
+    barrier = pltpu.get_barrier_semaphore()
+    for row, col in ((yp, c), (ym, c), (r, xp), (r, xm), (r, par)):
+        pl.semaphore_signal(barrier, inc=1, device_id={"row": row, "col": col}, device_id_type=MESH)
+    pl.semaphore_wait(barrier, 5)
+    start("rp+", "rp-", "up+", "up-", "rpp")
+    rp_in.start()
+    up_in.start()
+    w_in.start()
+    zero[...] = jnp.zeros_like(zero)
+
+    def at(j, k):
+        return (k, j % row_devs, pl.ds((j // row_devs) * blk, blk))
+
+    fwd_k = min(col_devs - 2, -(-9 * nq // 14))
+    end_k = min(col_devs - 1, nq + 1)
+    sd_in[0].wait()
+    dblk[...] = sd[at(0, 0)]
+
+    @pl.loop(0, col_devs)
+    def _(k):
+        lfac, inv = chol_inv(dblk[...])
+        dblk[...] = lfac
+        linv[k] = inv_operands(inv)
+        for kk in range(col_devs):
+            @pl.when(k == kk)
+            def _():
+                chain_rest(kk, at, sd_in, sd, dblk, linv, bsd, blk, col_devs)
+                if kk == fwd_k:
+                    got("rp+")
+                    start("rpf+", "rpr1")
+                    got("rp-")
+                    start("rpf-", "rpr2")
+                    got("up+")
+                    start("upf+")
+                    got("up-")
+                    start("upf-")
+                if kk == end_k:
+                    got("rpf+")
+                    start("rpr3")
+                    got("rpf-")
+                    start("rpr4")
+
+    for tt in range(col_devs // row_devs):
+        val = sd[c, r, pl.ds(tt * blk, blk)]
+        sd[c, r, pl.ds(tt * blk, blk)] = jnp.where(tt * row_devs + r >= c, val, jnp.zeros_like(val))
+    d_out.start()
+    up_in.wait()
+    gone("up+", "up-")
+    z_out.start()
+    rp_in.wait()
+    got("rpp", "rpr1", "rpr2", "rpr3", "rpr4", "upf+", "upf-")
+    gone("rp+", "rp-", "rpp", "rpf+", "rpf-", "rpr1", "rpr2", "rpr3", "rpr4", "upf+", "upf-")
+    w_in.wait()
+
+    def stage_a():
+        got("sy+")
+        start("syf+")
+        got("sy-")
+        start("syf-")
+
+    def stage_b():
+        got("syf+", "syf-")
+        start("sx+lo", "sx-hi", "sx+hi", "sx-lo", "sxp")
+
+    def stage_c():
+        got("sx+lo")
+        start("sxf+", "sr1lo")
+        got("sx-hi")
+        start("sxf-", "sr2hi")
+
+    def stage_d():
+        got("sx+hi")
+        start("sr1hi")
+        got("sx-lo")
+        start("sr2lo")
+
+    def stage_e():
+        got("sxf+")
+        start("sr3lo")
+        got("sxf-")
+        start("sr3hi")
+
+    stages = [(2, stage_a), (3, stage_b), (5, stage_c), (7, stage_d), (10, stage_e)]
+
+    @pl.loop(0, nq)
+    def _(q):
         for k in range(col_devs):
             ops = linv[k]
-
-            @pl.loop(0, nr + nc)
-            def _(i):
-                sl = pl.ds(pl.multiple_of(i * blk, blk), blk)
-                cur = pan[k, sl]
-                if k:
-                    cur = cur - lax.dot_general(bpan[sl, :k * blk], bsd[k * blk:(k + 1) * blk, :k * blk], NT, preferred_element_type=F32)
-                low = solve_f32(cur, ops)
-                pan[k, sl] = low
-                bpan[sl, k * blk:(k + 1) * blk] = low.astype(BF16)
-        l_out = pltpu.make_async_copy(pan.at[c, pl.ds(0, nr * blk)], out_ref.at[pl.ds(row0 + h, nr * blk), pl.ds(col0, blk)], sems.at[1])
-        l_out.start()
-        w_in.wait()
-
-        @pl.loop(0, nr // 2)
-        def _(i):
-            sl = pl.ds(pl.multiple_of(i * 2 * blk, 2 * blk), 2 * blk)
-            w[sl] = w[sl] - lax.dot_general(bpan[sl], bpan[nr * blk:], NT, preferred_element_type=F32)
-        w_out = pltpu.make_async_copy(w, out_ref.at[pl.ds(row0 + h, nr * blk), pl.ds(col0 + blk, nc * blk)], sems.at[3])
-        w_out.start()
-        w_out.wait()
-        l_out.wait()
-        z_out.wait()
+            pan[k, q, pl.ds(h, blk)] = up[k % row_devs, pl.ds((k // row_devs) * blk, blk), pl.ds(pl.multiple_of(q * blk, blk), blk)].T
+            cur = pan[k, q]
+            if k:
+                cur = cur - lax.dot_general(bq[:, :k * blk], bsd[k * blk:(k + 1) * blk, :k * blk], NT, preferred_element_type=F32)
+            low = solve_f32(cur, ops)
+            pan[k, q] = low
+            bq[:, k * blk:(k + 1) * blk] = low.astype(BF16)
+        bi[q] = bq[:h]
+        bj[pl.ds(pl.multiple_of(q * blk, blk), blk)] = bq[h:]
+
+        @pl.when(q == 0)
+        def _():
+            own[...] = w[0, :, :blk] - lax.dot_general(bq[:h], bq[h:], NT, preferred_element_type=F32)
+            n_out.start()
+            n_out.wait()
+            start("sy+", "sy-")
+        for pos, fn in stages:
+            if pos < nq:
+                pl.when(q == pos)(fn)
+
+    l_out.start()
+
+    @pl.loop(0, nq)
+    def _(q):
+        w[q] = w[q] - lax.dot_general(bi[q], bj[...], NT, preferred_element_type=F32)
+        for pos, fn in stages:
+            if nq <= pos < 2 * nq:
+                pl.when(q == pos - nq)(fn)
+
+    w_out.start()
+    for pos, fn in stages:
+        if pos >= 2 * nq:
+            fn()
+    l_out.wait()
+    z_out.wait()
     d_out.wait()
-
-
-def factor(a2, parts, s, blk, row_devs, col_devs, nr, nc):
-    per = col_devs // row_devs
-    h = per * blk
+    got("sxp", "sr1lo", "sr1hi", "sr2lo", "sr2hi", "sr3lo", "sr3hi")
+    gone("sy+", "sy-", "syf+", "syf-", "sx+lo", "sx+hi", "sx-lo", "sx-hi", "sxp", "sxf+", "sxf-",
+         "sr1lo", "sr1hi", "sr2lo", "sr2hi", "sr3lo", "sr3hi")
+    w_out.wait()
+
+
+def fused(a3, sd, s, blk, row_devs, col_devs, nq):
+    h = (col_devs // row_devs) * blk
     anyspec = pl.BlockSpec(memory_space=pl.ANY)
     scratch = [
         pltpu.VMEM((col_devs, row_devs, h, blk), F32),
         pltpu.VMEM((blk, blk), F32),
         pltpu.VMEM((col_devs, 3 * blk, 2 * blk), BF16),
         pltpu.VMEM((col_devs * blk, col_devs * blk), BF16),
-        pltpu.VMEM((h, max(nc, 1) * blk), F32),
-        pltpu.SemaphoreType.DMA((5,)),
+        pltpu.VMEM((h, nq * blk), F32),
+        pltpu.VMEM((col_devs, nq, h + blk, blk), F32),
+        pltpu.VMEM((row_devs, h, nq * blk), F32),
+        pltpu.VMEM((nq, h, nq * blk), F32),
+        pltpu.VMEM((nq, h, col_devs * blk), BF16),
+        pltpu.VMEM((nq * blk, col_devs * blk), BF16),
+        pltpu.VMEM((h + blk, col_devs * blk), BF16),
+        pltpu.VMEM((h, blk), F32),
+        pltpu.SemaphoreType.DMA((32,)),
+        pltpu.SemaphoreType.DMA((32,)),
+        pltpu.SemaphoreType.DMA((8,)),
+        pltpu.SemaphoreType.DMA((col_devs,)),
     ]
-    if nc:
-        scratch += [
-            pltpu.VMEM((col_devs, (nr + nc) * blk, blk), F32),
-            pltpu.VMEM((row_devs, h, nc * blk), F32),
-            pltpu.VMEM((nr * blk, nc * blk), F32),
-            pltpu.VMEM(((nr + nc) * blk, col_devs * blk), BF16),
-        ]
     return pl.pallas_call(
-        functools.partial(factor_kernel, (s, blk, row_devs, col_devs, nr, nc)),
-        out_shape=jax.ShapeDtypeStruct(a2.shape, F32),
-        in_specs=[anyspec] * (1 + len(parts)),
-        out_specs=anyspec,
+        functools.partial(fused_kernel, (s, blk, row_devs, col_devs, nq)),
+        out_shape=[jax.ShapeDtypeStruct(a3.shape, F32), jax.ShapeDtypeStruct(sd.shape, F32)],
+        in_specs=[anyspec, anyspec],
+        out_specs=[anyspec, anyspec],
         scratch_shapes=scratch,
         input_output_aliases={} if s == 0 else {0: 0},
-        compiler_params=pltpu.CompilerParams(vmem_limit_bytes=60 * 1024 * 1024),
-        name=f"factor_{s}",
-    )(a2, *parts)
+        compiler_params=pltpu.CompilerParams(vmem_limit_bytes=60 * 1024 * 1024, collective_id=s + 1, has_side_effects=True),
+        name=f"fused_{s}",
+    )(a3, sd)
 
 
 def solution(mesh):
@@ -359,13 +560,13 @@
 
     def factor_local(a_loc):
         row_blocks, blk, local_cols = a_loc.shape
-        col_blocks = local_cols // blk
-        a2 = a_loc.reshape(row_blocks * blk, local_cols)
-        for s in range(col_blocks):
-            nr, nc = row_blocks - per * (s + 1), col_blocks - s - 1
-            parts = gather(a2, s, blk, row_devs, col_devs, nr, nc)
-            a2 = factor(a2, parts, s, blk, row_devs, col_devs, nr, nc)
-        return a2.reshape(row_blocks, blk, local_cols)
+        steps = local_cols // blk
+        (sd,) = gather(a_loc.reshape(row_blocks * blk, local_cols), 0, blk, row_devs, col_devs, 0, 0)
+        a3 = a_loc.reshape(steps, per * blk, local_cols)
+        for s in range(steps - 1):
+            a3, sd = fused(a3, sd, s, blk, row_devs, col_devs, steps - 1 - s)
+        a3 = last(a3, sd, steps - 1, blk, row_devs, col_devs)
+        return a3.reshape(row_blocks, blk, local_cols)
 
     spec = P(("batch", "row"), None, "col")
     return jax.shard_map(factor_local, mesh=mesh, in_specs=(spec,), out_specs=spec, check_vma=False)

time: 938 us -> 606 us (0.65)
  Pallas kernels: 931 us -> 598 us
    pallas_call x8 -> x1, Pallas kernels: 359 us -> 35 us  [gather(): pl.pallas_call(functools.partial(gather_kernel, (s, blk, row_devs, col_de...]
where the time goes in v2:
time: 606 us; the launch traced here: 598 us
  Pallas kernels  598 us (99%)
    pallas_call x7, Pallas kernels, fused(): pl.pallas_call(functools.partial(fused_kernel, (s, blk, row_devs, col_dev...  525 us
    pallas_call x1, Pallas kernels, last(): pl.pallas_call(functools.partial(last_kernel, (s, blk, row_devs, col_devs...  38.3 us
    pallas_call x1, Pallas kernels, gather(): pl.pallas_call(functools.partial(gather_kernel, (s, blk, row_devs, col_de...  35 us

profile of v2, /device:TPU:97, one launch (start us, length us, event | category | flops | bytes accessed | tf_op | source)
XLA Modules:
  0.0 598.5 jit_solution(9331602161169149689)
XLA Ops:
  0.0 35.0 %gather_0.1.sd_hbm = f32[8,4,256,128]{3,2,1,0:T(8,128)} custom-call(f32[2048,1024]{1,0:T(8,128)} %bitcast.3), custom_call_target="tpu_custom_call" | custom-call | tf_op jit(solution)/shard_map/gather_0/pallas_call | solution.py:221
  35.0 82.7 %fused_0.1 = (f32[8,256,1024]{2,1,0:T(8,128)}, f32[8,4,256,128]{3,2,1,0:T(8,128)}) custom-call(f32[8,256,1024]{2,1,0:T(8,128)} %bitcast.4, f32[8,4,256,128]{3,2,1,0:T(8,128)} %gather_0.1.sd_hbm), custom_call_target="tpu_custom_call" | custom-call | tf_op jit(solution)/shard_map/fused_0/pallas_call | solution.py:544
  117.7 78.0 %fused_1.1 = (f32[8,256,1024]{2,1,0:T(8,128)}, f32[8,4,256,128]{3,2,1,0:T(8,128)}) custom-call(f32[8,256,1024]{2,1,0:T(8,128)} %get-tuple-element.19.a_ref, f32[8,4,256,128]{3,2,1,0:T(8,128)} %get-tuple-element.20.sd_hbm), custom_call_target="tpu_custom_call", output_to_operand_aliasing={{0}: (0, {})} | custom-call | tf_op jit(solution)/shard_map/fused_1/pallas_call | solution.py:544
  195.7 73.5 %fused_2.1 = (f32[8,256,1024]{2,1,0:T(8,128)}, f32[8,4,256,128]{3,2,1,0:T(8,128)}) custom-call(f32[8,256,1024]{2,1,0:T(8,128)} %get-tuple-element.21.a_ref, f32[8,4,256,128]{3,2,1,0:T(8,128)} %get-tuple-element.22.sd_hbm), custom_call_target="tpu_custom_call", output_to_operand_aliasing={{0}: (0, {})} | custom-call | tf_op jit(solution)/shard_map/fused_2/pallas_call | solution.py:544
  269.2 74.0 %fused_3.1 = (f32[8,256,1024]{2,1,0:T(8,128)}, f32[8,4,256,128]{3,2,1,0:T(8,128)}) custom-call(f32[8,256,1024]{2,1,0:T(8,128)} %get-tuple-element.23.a_ref, f32[8,4,256,128]{3,2,1,0:T(8,128)} %get-tuple-element.24.sd_hbm), custom_call_target="tpu_custom_call", output_to_operand_aliasing={{0}: (0, {})} | custom-call | tf_op jit(solution)/shard_map/fused_3/pallas_call | solution.py:544
  343.3 73.8 %fused_4.1 = (f32[8,256,1024]{2,1,0:T(8,128)}, f32[8,4,256,128]{3,2,1,0:T(8,128)}) custom-call(f32[8,256,1024]{2,1,0:T(8,128)} %get-tuple-element.25.a_ref, f32[8,4,256,128]{3,2,1,0:T(8,128)} %get-tuple-element.26.sd_hbm), custom_call_target="tpu_custom_call", output_to_operand_aliasing={{0}: (0, {})} | custom-call | tf_op jit(solution)/shard_map/fused_4/pallas_call | solution.py:544
  417.1 70.7 %fused_5.1 = (f32[8,256,1024]{2,1,0:T(8,128)}, f32[8,4,256,128]{3,2,1,0:T(8,128)}) custom-call(f32[8,256,1024]{2,1,0:T(8,128)} %get-tuple-element.27.a_ref, f32[8,4,256,128]{3,2,1,0:T(8,128)} %get-tuple-element.28.sd_hbm), custom_call_target="tpu_custom_call", output_to_operand_aliasing={{0}: (0, {})} | custom-call | tf_op jit(solution)/shard_map/fused_5/pallas_call | solution.py:544
  487.8 71.8 %fused_6.1 = (f32[8,256,1024]{2,1,0:T(8,128)}, f32[8,4,256,128]{3,2,1,0:T(8,128)}) custom-call(f32[8,256,1024]{2,1,0:T(8,128)} %get-tuple-element.29.a_ref, f32[8,4,256,128]{3,2,1,0:T(8,128)} %get-tuple-element.30.sd_hbm), custom_call_target="tpu_custom_call", output_to_operand_aliasing={{0}: (0, {})} | custom-call | tf_op jit(solution)/shard_map/fused_6/pallas_call | solution.py:544
  559.6 38.3 %last_7.1 = f32[8,256,1024]{2,1,0:T(8,128)} custom-call(f32[8,256,1024]{2,1,0:T(8,128)} %get-tuple-element.31.a_ref, f32[8,4,256,128]{3,2,1,0:T(8,128)} %get-tuple-element.32.sd_hbm), custom_call_target="tpu_custom_call" | custom-call | tf_op jit(solution)/shard_map/last_7/pallas_call | solution.py:275

commit v3 on v2

--- a/solution.py
+++ b/solution.py
@@ -15,48 +15,64 @@
 
 def chol_inv(blk):
     n = blk.shape[0]
+    groups = n // SUB
     lane = lax.broadcasted_iota(jnp.int32, (SUB, n), 1)
     sub = lax.broadcasted_iota(jnp.int32, (SUB, n), 0)
-    t = blk
-    lout = jnp.zeros((n, n), F32)
-    l_rows, inv_rows = [], []
-    for p in range(n // SUB):
+    ident = lane - sub
+    spread = lambda v: jnp.broadcast_to(v, (SUB, n))
+    pull = lambda rows, at: jnp.concatenate([spread(rows[:, at + m:at + m + 1])[None] for m in range(SUB)], axis=0)
+    t0, t1, rest = blk[:SUB], blk[SUB:2 * SUB], blk[2 * SUB:]
+    upper, diag, inv_rows = [], [], []
+    c0, c1 = pull(t0, 0), pull(t1, 0)
+    for p in range(groups):
         base = p * SUB
-        rows = n - base
-        more = rows > SUB
-        cols = [jnp.broadcast_to(t[:, base + m:base + m + 1], (rows, n)) for m in range(SUB)]
-        c0 = [c[:SUB] for c in cols]
         inside = (lane >= base) & (lane < base + SUB)
-        t0 = jnp.where(inside, jnp.where(lane == sub + base, 1.0, 0.0), t[:SUB])
-        o0 = lout[:SUB]
-        if more:
-            c1 = [c[SUB:] for c in cols]
-            lane1 = lax.broadcasted_iota(jnp.int32, (rows - SUB, n), 1)
-            t1 = jnp.where((lane1 >= base) & (lane1 < base + SUB), 0.0, t[SUB:])
-            o1 = lout[SUB:]
+        t0 = jnp.where(inside, jnp.where(ident == base, 1.0, 0.0), t0)
+        if t1 is not None:
+            t1 = jnp.where(inside, 0.0, t1)
+        if rest is not None:
+            wide = jnp.concatenate([inside] * (rest.shape[0] // SUB), axis=0)
+            rest = jnp.where(wide, 0.0, rest)
+        o = jnp.zeros((SUB, n), F32)
+        urows = []
         for j in range(SUB):
-            r = lax.rsqrt(jnp.broadcast_to(c0[j][j:j + 1], (SUB, n)))
+            r = lax.rsqrt(spread(c0[j, j:j + 1]))
             l0 = c0[j] * r
             l0m = jnp.where(sub > j, l0, 0.0)
-            urow = jnp.broadcast_to(t0[j:j + 1], (SUB, n)) * r
-            o0 = jnp.where((lane == base + j) & (sub >= j), l0, o0)
+            urow = spread(t0[j:j + 1]) * r
+            urows.append(urow)
             t0 = jnp.where(sub == j, urow, t0 - l0m * urow)
-            spl = {m: jnp.broadcast_to(c0[m][j:j + 1], (SUB, n)) * r for m in range(j + 1, SUB)}
-            for m in range(j + 1, SUB):
-                c0[m] = c0[m] - l0m * spl[m]
-            if more:
-                reps = (rows - SUB) // SUB
-                wide = lambda v: jnp.concatenate([v] * reps, axis=0) if reps > 1 else v
-                l1 = c1[j] * wide(r)
-                o1 = jnp.where(lane1 == base + j, l1, o1)
-                t1 = t1 - l1 * wide(urow)
-                for m in range(j + 1, SUB):
-                    c1[m] = c1[m] - l1 * wide(spl[m])
+            o = jnp.where((lane == base + j) & (sub >= j), l0, o)
+            if j + 1 < SUB:
+                spl = jnp.broadcast_to(c0[j + 1:, j:j + 1], (SUB - 1 - j, SUB, n)) * r[None]
+                c0 = jnp.concatenate([c0[:j + 1], c0[j + 1:] - l0m[None] * spl], axis=0)
+            if t1 is not None:
+                l1 = c1[j] * r
+                t1 = t1 - l1 * urow
+                if j + 1 < SUB:
+                    c1 = jnp.concatenate([c1[:j + 1], c1[j + 1:] - l1[None] * spl], axis=0)
         inv_rows.append(jnp.where(lane < base + SUB, t0, 0.0))
-        l_rows.append(o0)
-        if more:
-            t, lout = t1, o1
-    return jnp.concatenate(l_rows, axis=0), jnp.concatenate(inv_rows, axis=0)
+        upper.append(jnp.where(lane >= base + SUB, t0, 0.0))
+        diag.append(o)
+        if t1 is None:
+            break
+        c0 = pull(t1, base + SUB)
+        nxt = None
+        if rest is not None:
+            ut = t0.T[base + 2 * SUB:]
+            nxt, more = rest[:SUB], rest[SUB:]
+            for j in range(SUB):
+                nxt = nxt - spread(ut[:SUB, j:j + 1]) * urows[j]
+            c1 = pull(nxt, base + SUB)
+            rest = None
+            if more.shape[0]:
+                for j in range(SUB):
+                    tall = jnp.concatenate([urows[j]] * (more.shape[0] // SUB), axis=0)
+                    more = more - jnp.broadcast_to(ut[SUB:, j:j + 1], more.shape) * tall
+                rest = more
+        t0, t1 = t1, nxt
+    lfac = jnp.concatenate(upper, axis=0).T + jnp.concatenate(diag, axis=0)
+    return lfac, jnp.concatenate(inv_rows, axis=0)
 
 
 def split3(x):

time: 606 us -> 615 us (1.015)
  Pallas kernels: 598 us -> 606 us
    pallas_call x7, Pallas kernels: 525 us -> 532 us  [fused(): pl.pallas_call(functools.partial(fused_kernel, (s, blk, row_devs, col_dev...]
where the time goes in v3:
time: 615 us; the launch traced here: 607 us
  Pallas kernels  606 us (99%)
    pallas_call x7, Pallas kernels, fused(): pl.pallas_call(functools.partial(fused_kernel, (s, blk, row_devs, col_dev...  532 us
    pallas_call x1, Pallas kernels, last(): pl.pallas_call(functools.partial(last_kernel, (s, blk, row_devs, col_devs...  39.4 us
    pallas_call x1, Pallas kernels, gather(): pl.pallas_call(functools.partial(gather_kernel, (s, blk, row_devs, col_de...  35 us

profile of v3, /device:TPU:97, one launch (start us, length us, event | category | flops | bytes accessed | tf_op | source)
XLA Modules:
  0.0 607.0 jit_solution(2638134777101360520)
XLA Ops:
  0.0 35.0 %gather_0.1.sd_hbm = f32[8,4,256,128]{3,2,1,0:T(8,128)} custom-call(f32[2048,1024]{1,0:T(8,128)} %bitcast.3), custom_call_target="tpu_custom_call" | custom-call | tf_op jit(solution)/shard_map/gather_0/pallas_call | solution.py:237
  35.0 83.5 %fused_0.1 = (f32[8,256,1024]{2,1,0:T(8,128)}, f32[8,4,256,128]{3,2,1,0:T(8,128)}) custom-call(f32[8,256,1024]{2,1,0:T(8,128)} %bitcast.4, f32[8,4,256,128]{3,2,1,0:T(8,128)} %gather_0.1.sd_hbm), custom_call_target="tpu_custom_call" | custom-call | tf_op jit(solution)/shard_map/fused_0/pallas_call | solution.py:560
  118.5 79.2 %fused_1.1 = (f32[8,256,1024]{2,1,0:T(8,128)}, f32[8,4,256,128]{3,2,1,0:T(8,128)}) custom-call(f32[8,256,1024]{2,1,0:T(8,128)} %get-tuple-element.19.a_ref, f32[8,4,256,128]{3,2,1,0:T(8,128)} %get-tuple-element.20.sd_hbm), custom_call_target="tpu_custom_call", output_to_operand_aliasing={{0}: (0, {})} | custom-call | tf_op jit(solution)/shard_map/fused_1/pallas_call | solution.py:560
  197.7 74.6 %fused_2.1 = (f32[8,256,1024]{2,1,0:T(8,128)}, f32[8,4,256,128]{3,2,1,0:T(8,128)}) custom-call(f32[8,256,1024]{2,1,0:T(8,128)} %get-tuple-element.21.a_ref, f32[8,4,256,128]{3,2,1,0:T(8,128)} %get-tuple-element.22.sd_hbm), custom_call_target="tpu_custom_call", output_to_operand_aliasing={{0}: (0, {})} | custom-call | tf_op jit(solution)/shard_map/fused_2/pallas_call | solution.py:560
  272.3 75.1 %fused_3.1 = (f32[8,256,1024]{2,1,0:T(8,128)}, f32[8,4,256,128]{3,2,1,0:T(8,128)}) custom-call(f32[8,256,1024]{2,1,0:T(8,128)} %get-tuple-element.23.a_ref, f32[8,4,256,128]{3,2,1,0:T(8,128)} %get-tuple-element.24.sd_hbm), custom_call_target="tpu_custom_call", output_to_operand_aliasing={{0}: (0, {})} | custom-call | tf_op jit(solution)/shard_map/fused_3/pallas_call | solution.py:560
  347.4 74.9 %fused_4.1 = (f32[8,256,1024]{2,1,0:T(8,128)}, f32[8,4,256,128]{3,2,1,0:T(8,128)}) custom-call(f32[8,256,1024]{2,1,0:T(8,128)} %get-tuple-element.25.a_ref, f32[8,4,256,128]{3,2,1,0:T(8,128)} %get-tuple-element.26.sd_hbm), custom_call_target="tpu_custom_call", output_to_operand_aliasing={{0}: (0, {})} | custom-call | tf_op jit(solution)/shard_map/fused_4/pallas_call | solution.py:560
  422.3 71.8 %fused_5.1 = (f32[8,256,1024]{2,1,0:T(8,128)}, f32[8,4,256,128]{3,2,1,0:T(8,128)}) custom-call(f32[8,256,1024]{2,1,0:T(8,128)} %get-tuple-element.27.a_ref, f32[8,4,256,128]{3,2,1,0:T(8,128)} %get-tuple-element.28.sd_hbm), custom_call_target="tpu_custom_call", output_to_operand_aliasing={{0}: (0, {})} | custom-call | tf_op jit(solution)/shard_map/fused_5/pallas_call | solution.py:560
  494.1 73.0 %fused_6.1 = (f32[8,256,1024]{2,1,0:T(8,128)}, f32[8,4,256,128]{3,2,1,0:T(8,128)}) custom-call(f32[8,256,1024]{2,1,0:T(8,128)} %get-tuple-element.29.a_ref, f32[8,4,256,128]{3,2,1,0:T(8,128)} %get-tuple-element.30.sd_hbm), custom_call_target="tpu_custom_call", output_to_operand_aliasing={{0}: (0, {})} | custom-call | tf_op jit(solution)/shard_map/fused_6/pallas_call | solution.py:560
  567.0 39.4 %last_7.1 = f32[8,256,1024]{2,1,0:T(8,128)} custom-call(f32[8,256,1024]{2,1,0:T(8,128)} %get-tuple-element.31.a_ref, f32[8,4,256,128]{3,2,1,0:T(8,128)} %get-tuple-element.32.sd_hbm), custom_call_target="tpu_custom_call" | custom-call | tf_op jit(solution)/shard_map/last_7/pallas_call | solution.py:291
